TPU v7x, 32 devices: a whole 2x2x4 slice. The times are simulated.
32 devices in a mesh: grp: 2 (over y), tile: 4 (over z), coil: 2 (over x), spk: 2 (over core).
Axes of the slice: x: 2, y: 2, z: 4, core: 2. Of those that a mesh axis runs over, the one named last changes fastest.
Arguments:
- coil_maps: float32 [2, 512, 2, 256], P('coil', ('grp', 'tile', 'spk')), parts along dimension 1, may hold values from -6 to 6
- kspace_data: bfloat16 [2, 128, 2, 256], P('coil', ('grp', 'tile', 'spk')), parts along dimension 1, may hold values from -24 to 24
- interp_weights: bfloat16 [128, 6, 256], P(('grp', 'tile', 'spk')), parts along dimension 0, may hold values from 0.099609375 to 1
- sample_bins: int32 [128, 256], P(('grp', 'tile', 'spk')), parts along dimension 0, may hold values from 0 to 65535, as said below
- spoke_count: int32 [16], P(('grp', 'tile', 'spk')), parts along dimension 0, may hold values from 1 to 8, 32 in all
- thresholds: float32 [3], replicated, may hold values from 0.05 to 0.3
Outputs:
- image: float32 [512, 2, 256], P(('grp', 'tile', 'spk')), parts along dimension 0
There are 2 independent parts, one for each index of `grp`. A program takes and returns all parts, laid end to end along the dimension named above; an argument that names none is the same for every part. Nothing has to cross between parts.
Inputs may be any that keep to these rules, and one draw needn't show every extreme that they name: `sample_bins`: sample k of each spoke lies on a straight line through cell (128, 128), at offset k - 128 along the spoke's direction, coordinates taken modulo 256. `spoke_count`: each independent slice has its own 8 counts, and the whole array holds one such block of counts per slice. The 8 counts of each slice sum to 32. In every draw, at least one device of each slice holds 8 live spokes. A device's live spokes are its first ones.
All inputs are finite; a program needn't handle non-finite values.
Results may differ from a plain program's by a relative error of at most 0.0016.
Values may be sent and summed in bfloat16 or wider, within the bound.
A program may use at most 64 MiB of HBM per device.

v0:
```python
import math

import jax
import jax.numpy as jnp
from jax import lax
from jax.sharding import PartitionSpec as P

N = 256
RO = 256
SPK_DEV = 8
LEVELS = 3
ITERS = 4


HIGH = lax.Precision.HIGHEST
STEP_SIZE = 0.5
RSQRT2 = 0.7071067811865476


def dft_table(length, direction):
    positions = jnp.arange(length, dtype=jnp.int32)
    phases = positions[:, None] * positions[None, :] % length
    angles = phases.astype(jnp.float32) * jnp.float32(2.0 * math.pi / length)
    norm_scale = 1.0 / math.sqrt(length)
    cosine = jnp.cos(angles) * norm_scale
    sine_tab = jnp.sin(angles) * norm_scale
    top_rows = jnp.stack([cosine, -direction * sine_tab], axis=1)
    bottom = jnp.stack([direction * sine_tab, cosine], axis=1)
    return jnp.stack([top_rows, bottom], axis=0)


def haar_matrix(length, levels):
    haar_mat = jnp.eye(length, dtype=jnp.float32)
    positions = jnp.arange(length, dtype=jnp.int32)
    out_i = positions[:, None]
    in_j = positions[None, :]
    for level_num in range(levels):
        span_len = length >> level_num
        half_len = span_len // 2
        low_hit = (out_i < half_len) & ((in_j == 2 * out_i) | (in_j == 2 * out_i + 1))
        high_pos = out_i - half_len
        high_hit = (
            (out_i >= half_len)
            & (out_i < span_len)
            & ((in_j == 2 * high_pos) | (in_j == 2 * high_pos + 1))
        )
        sign_val = jnp.where(in_j == 2 * high_pos + 1, -1.0, 1.0)
        step_mat = jnp.where(low_hit, RSQRT2, jnp.where(high_hit, sign_val * RSQRT2, 0.0))
        step_mat = step_mat + jnp.where((out_i >= span_len) & (in_j == out_i), 1.0, 0.0)
        haar_mat = jnp.dot(step_mat.astype(jnp.float32), haar_mat, precision=HIGH)
    return haar_mat


def haar_labels(length, levels):
    positions = jnp.arange(length, dtype=jnp.int32)
    band_label = jnp.ones((length,), jnp.int32)
    for level_num in range(1, levels + 1):
        band_label = band_label + (positions < length >> level_num).astype(jnp.int32)
    return band_label


def wavelet_shrink(target, thresholds, levels):
    row_count, pair_dim, col_count = target.shape
    block_len = 2**levels
    row_haar = haar_matrix(block_len, levels)
    col_haar = haar_matrix(col_count, levels)
    grouped = target.reshape(row_count // block_len, block_len, pair_dim, col_count)
    coeffs = jnp.einsum("ij,gjpc->gipc", row_haar, grouped, precision=HIGH)
    coeffs = jnp.einsum("gipc,kc->gipk", coeffs, col_haar, precision=HIGH)
    band_min = jnp.minimum(
        haar_labels(block_len, levels)[:, None], haar_labels(col_count, levels)[None, :]
    )
    active = band_min <= levels
    limits = jnp.ones(band_min.shape, jnp.float32)
    for level_num in range(levels):
        limits = jnp.where(band_min == level_num + 1, thresholds[level_num], limits)
    magnitude = jnp.sqrt(coeffs[:, :, 0] ** 2 + coeffs[:, :, 1] ** 2)
    factor = jnp.maximum(magnitude - limits, 0.0) / jnp.maximum(magnitude, limits)
    factor = jnp.where(active, factor, 1.0)
    shrunk = coeffs * factor[:, :, None, :]
    restored = jnp.einsum("gipk,kc->gipc", shrunk, col_haar, precision=HIGH)
    restored = jnp.einsum("ij,gipc->gjpc", row_haar, restored, precision=HIGH)
    return restored.reshape(row_count, pair_dim, col_count)


def complex_mul(left, right):
    real_part = left[:, 0] * right[:, 0] - left[:, 1] * right[:, 1]
    imag_part = left[:, 0] * right[:, 1] + left[:, 1] * right[:, 0]
    return jnp.stack([real_part, imag_part], axis=1)


def conj_mul(left, right):
    real_part = left[:, 0] * right[:, 0] + left[:, 1] * right[:, 1]
    imag_part = left[:, 0] * right[:, 1] - left[:, 1] * right[:, 0]
    return jnp.stack([real_part, imag_part], axis=1)


def interp_tables(load_bins, load_interp):
    grid_ids = jnp.arange(N, dtype=jnp.int32)
    row_bins = load_bins // N
    col_bins = load_bins % N
    zero_val = jnp.zeros((), jnp.bfloat16)
    row_table = jnp.zeros((load_bins.shape[0], load_bins.shape[1], N), jnp.bfloat16)
    col_table = jnp.zeros((load_bins.shape[0], N, load_bins.shape[1]), jnp.bfloat16)
    for tap_index in range(3):
        row_hit = grid_ids[None, None, :] == ((row_bins + tap_index - 1) % N)[:, :, None]
        row_table = row_table + jnp.where(
            row_hit, load_interp[:, tap_index, :][:, :, None], zero_val
        )
        col_hit = grid_ids[None, :, None] == ((col_bins + tap_index - 1) % N)[:, None, :]
        col_table = col_table + jnp.where(
            col_hit, load_interp[:, 3 + tap_index, :][:, None, :], zero_val
        )
    return (row_table, col_table)


def local(coil_maps, kspace_data, interp_weights, sample_bins, spoke_count, thresholds):
    blocks = lax.axis_size(("tile", "spk"))
    row_count = coil_maps.shape[1]
    live_total = blocks * SPK_DEV // 2
    coil_sens = coil_maps[0]
    measured = kspace_data[0]
    my_index = lax.axis_index(("tile", "spk"))
    counts = lax.all_gather(spoke_count, ("tile", "spk"), axis=0, tiled=True)
    prefix = jnp.cumsum(counts) - counts
    per_peer = -(-SPK_DEV // blocks)
    peer_ids = jnp.arange(blocks, dtype=jnp.int32)
    first_slot = (peer_ids - prefix[my_index]) % blocks
    slot_index = first_slot[:, None] + blocks * jnp.arange(per_peer, dtype=jnp.int32)[None, :]
    picked = jnp.clip(slot_index, 0, SPK_DEV - 1)
    values = jnp.concatenate([measured, interp_weights], axis=1)
    got_values = lax.all_to_all(
        values[picked], ("tile", "spk"), split_axis=0, concat_axis=0, tiled=True
    )
    got_bins = lax.all_to_all(
        sample_bins[picked], ("tile", "spk"), split_axis=0, concat_axis=0, tiled=True
    )
    my_share = SPK_DEV // 2
    wanted = my_index + blocks * jnp.arange(my_share, dtype=jnp.int32)
    source = jnp.sum((prefix[None, :] <= wanted[:, None]).astype(jnp.int32), axis=1) - 1
    depth_at = (wanted - prefix[source]) // blocks
    loaded = got_values[source, depth_at]
    load_bins = got_bins[source, depth_at]
    load_data = loaded[:, 0:2]
    load_interp = loaded[:, 2:8]
    row_table, col_table = interp_tables(load_bins, load_interp)
    n_load = row_table.shape[0]
    offset = jnp.abs(jnp.arange(RO, dtype=jnp.int32) - RO // 2).astype(jnp.float32)
    density = (offset + 0.5) * (N / (3.0 * RO * live_total))
    target_data = load_data.astype(jnp.float32)
    fwd_table = dft_table(N, 1.0)
    inv_table = dft_table(N, -1.0)

    def grid_rows(weighted):

        def grid_term(row_start, piece_rows):

            def grid_one_spoke(spoke_index, partial_value):
                row_one = lax.dynamic_index_in_dim(row_table, spoke_index, 0, keepdims=False)
                col_one = lax.dynamic_index_in_dim(col_table, spoke_index, 0, keepdims=False)
                col_slice = col_one.astype(jnp.float32)
                residue = lax.dynamic_index_in_dim(weighted, spoke_index, 0, keepdims=False)
                smeared = (col_slice[:, None, :] * residue[None, :, :]).astype(jnp.bfloat16)
                added = jnp.dot(
                    smeared.reshape(piece_rows * 2, RO), row_one, preferred_element_type=jnp.float32
                )
                return partial_value + added.reshape(piece_rows, 2, N)

            return lax.fori_loop(
                0, my_share, grid_one_spoke, jnp.zeros((piece_rows, 2, N), jnp.float32)
            )

        return grid_term

    estimate = jnp.zeros((row_count, 2, N), jnp.float32)
    for iteration in range(ITERS):
        if iteration == 0:
            weighted = -density[None, None, :] * target_data
        else:
            coil_image = complex_mul(coil_sens, estimate)
            half_done = jnp.einsum("rpc,pcqv->rqv", coil_image, fwd_table, precision=HIGH)
            turned = lax.all_to_all(
                half_done, ("tile", "spk"), split_axis=2, concat_axis=0, tiled=True
            )
            kspace = jnp.einsum("rpv,prqu->vqu", turned, fwd_table, precision=HIGH).astype(
                jnp.bfloat16
            )
            piece = lax.all_gather(kspace, ("tile", "spk"), axis=0, tiled=True)
            fold_piece_rows = piece.shape[0]
            flat_piece = piece.reshape(fold_piece_rows * 2, N)

            def fold_one_spoke(spoke_index, partial_value):
                row_one = lax.dynamic_index_in_dim(row_table, spoke_index, 0, keepdims=False)
                col_one = lax.dynamic_index_in_dim(col_table, spoke_index, 0, keepdims=False)
                inner_sum = lax.dot_general(
                    flat_piece,
                    row_one,
                    (((1,), (1,)), ((), ())),
                    preferred_element_type=jnp.float32,
                )
                inner_sum = inner_sum.reshape(fold_piece_rows, 2, RO)
                col_slice = col_one.astype(jnp.float32)
                added = jnp.sum(inner_sum * col_slice[:, None, :], axis=0)
                current = lax.dynamic_index_in_dim(partial_value, spoke_index, 0, keepdims=False)
                return lax.dynamic_update_index_in_dim(
                    partial_value, current + added, spoke_index, 0
                )

            sample_model = lax.fori_loop(
                0, my_share, fold_one_spoke, jnp.zeros((n_load, 2, RO), jnp.float32)
            )
            weighted = density[None, None, :] * (sample_model - target_data)
        grid_term = grid_rows(weighted)
        owned_rows = lax.psum_scatter(
            grid_term(jnp.int32(0), row_count * lax.axis_size(("tile", "spk"))),
            ("tile", "spk"),
            scatter_dimension=0,
            tiled=True,
        )
        partial_back = jnp.einsum("vpu,puqr->vqr", owned_rows, inv_table, precision=HIGH)
        returned = lax.all_to_all(
            partial_back, ("tile", "spk"), split_axis=2, concat_axis=0, tiled=True
        )
        coil_back = jnp.einsum("vpr,pvqc->rqc", returned, inv_table, precision=HIGH)
        gradient = lax.psum(conj_mul(coil_sens, coil_back), "coil")
        estimate = wavelet_shrink(estimate - STEP_SIZE * gradient, thresholds, LEVELS)
    return estimate


def solution(mesh):
    placed = (
        P("coil", ("grp", "tile", "spk"), None, None),
        P("coil", ("grp", "tile", "spk"), None, None),
        P(("grp", "tile", "spk"), None, None),
        P(("grp", "tile", "spk"), None),
        P(("grp", "tile", "spk")),
        P(),
    )
    return jax.shard_map(
        local,
        mesh=mesh,
        in_specs=placed,
        out_specs=P(("grp", "tile", "spk"), None, None),
        check_vma=False,
    )
```

profile of v0, /device:TPU:11, one launch (start us, length us, event | category | flops | bytes accessed | tf_op | source)
XLA Modules:
  0.0 509.4 jit_solution(6684872715194408570)
XLA Ops:
  9.2 6.5 %all-reduce = s32[8]{0:T(128)S(1)} all-reduce(s32[8]{0:T(128)S(1)} %dynamic-update-slice), channel_id=1, replica_groups=mesh['grp'=2,'tile'=4,'coil'=2,'spk'=2] {'tile','spk'}, use_global_device_ids=true, to_apply=%add | all-reduce | flops 8 | bytes 64
  18.3 6.6 %all-to-all-start = ((s32[8,1,256]{2,1,0:T(1,128)}), s32[8,1,256]{2,1,0:T(1,128)S(1)}, u32[]{:S(2)}, u32[]{:S(2)}) async-start(s32[8,1,256]{2,1,0:T(1,128)} %copy.115), calls=%async_computation | async-start | bytes 16384 | tf_op jit(solution)/shard_map/all_to_all | solution.py:135
  33.3 5.1 %all-to-all-start.1 = ((bf16[8,1,8,256]{3,2,1,0:T(8,128)(2,1)}), bf16[8,1,8,256]{3,2,1,0:T(8,128)(2,1)S(1)}, u32[]{:S(2)}, u32[]{:S(2)}) async-start(bf16[8,1,8,256]{3,2,1,0:T(8,128)(2,1)} %bitcast.26), calls=%async_computation.1 | async-start | bytes 65536 | tf_op jit(solution)/shard_map/all_to_all | solution.py:132
  39.1 3.4 all-to-all-done.1
  45.2 7.5 %while.98 = (s32[]{:T(128)}, f32[256,2,256]{2,0,1:T(8,128)}, bf16[4,256,256]{2,1,0:T(8,128)(2,1)S(1)}, f32[4,2,256]{2,1,0:T(2,128)S(1)}, bf16[4,256,256]{2,1,0:T(8,128)(2,1)S(1)}, /*index=5*/s32[]{:T(128)}, s32[]{:T(128)}) while((s32[]{:T(128)}, f32[256,2,256]{2,0,1:T(8,128)}, bf16[4,256,256]{2,1,0:T(8,128)(2,1)S(1)}, ...), condition=%wide.region_3.4_spmd.clone, body=%wide.region_2.3_spmd.clone.sunk | while | flops 67698688 | bytes 1841251 | solution.py:169
  46.4 2.1 convolution_add_fusion.8
  48.5 2.1 convolution_add_fusion.8
  50.6 2.1 convolution_add_fusion.8
  54.6 2.7 select_select_fusion
  58.1 18.5 %reduce-scatter.5.cloned.1.call-done = f32[32,2,256]{2,0,1:T(8,128)} async-done(((f32[256,2,256]{2,0,1:T(8,128)}), f32[32,2,256]{2,0,1:T(8,128)}) %reduce-scatter.5.cloned.1.call-update) | async-done | bytes 65552 | tf_op jit(solution)/shard_map/reduce_scatter | solution.py:214
  79.0 1.9 reshape.880
  80.9 10.9 %all-to-all-start.2 = ((f32[8,1,2048]{2,1,0:T(1,128)}), f32[8,1,2048]{2,1,0:T(1,128)S(1)}, u32[]{:S(2)}, u32[]{:S(2)}) async-start(f32[8,1,2048]{2,1,0:T(1,128)} %reshape.880), calls=%async_computation.3 | async-start | bytes 131072 | tf_op jit(solution)/shard_map/all_to_all | solution.py:221
  93.8 2.3 all-to-all-done.2
  99.9 1.8 copy.229
  105.1 18.0 %all-reduce.6.cloned.1.call-done = f32[32,2,256]{2,0,1:T(8,128)} async-done(((f32[32,2,256]{2,0,1:T(8,128)}), f32[32,2,256]{2,0,1:T(8,128)}) %all-reduce.6.cloned.1.call-update) | async-done | bytes 65552 | tf_op jit(solution)/shard_map/psum | solution.py:225
  126.7 1.7 copy.125
  128.4 1.9 reshape.882
  130.2 5.9 %all-to-all-start.3 = ((f32[8,1,2048]{2,1,0:T(1,128)}), f32[8,1,2048]{2,1,0:T(1,128)}, u32[]{:S(2)}, u32[]{:S(2)}) async-start(f32[8,1,2048]{2,1,0:T(1,128)} %reshape.882), calls=%async_computation.4 | async-start | bytes 131072 | tf_op jit(solution)/shard_map/all_to_all | solution.py:182
  136.7 3.8 all-to-all-done.3
  140.5 2.2 reduce.1
  142.7 1.8 reshape.883
  144.5 1.8 copy.228
  146.3 1.7 reshape.848
  149.6 13.1 %all_gather.13 = bf16[256,2,256]{2,0,1:T(8,128)(2,1)S(1)} all-gather(bf16[32,2,256]{2,0,1:T(8,128)(2,1)S(1)} %fusion.32), channel_id=1, replica_groups=mesh['grp'=2,'tile'=4,'coil'=2,'spk'=2] {'tile','spk'}, dimensions={0}, use_global_device_ids=true | all-gather | bytes 294912 | tf_op jit(solution)/shard_map/all_gather | solution.py:188
  163.7 12.7 %while.95 = (s32[]{:T(128)}, f32[4,2,256]{2,1,0:T(2,128)}, bf16[4,256,256]{2,1,0:T(8,128)(2,1)S(1)}, bf16[512,256]{1,0:T(8,128)(2,1)S(1)}, bf16[4,256,256]{2,1,0:T(8,128)(2,1)S(1)}, /*index=5*/s32[]{:T(128)}) while((s32[]{:T(128)}, f32[4,2,256]{2,1,0:T(2,128)}, bf16[4,256,256]{2,1,0:T(8,128)(2,1)S(1)}, bf16[512,256]{1,0:T(8,128)(2,1)S(1)}, ...), condition=%wide.region_8.9_spmd, body=%wide.region_6.8_spmd.sunk | while | flops 67436544 | bytes 6300293 | solution.py:209
  177.8 7.5 %while.99 = (s32[]{:T(128)}, f32[256,2,256]{2,0,1:T(8,128)}, bf16[4,256,256]{2,1,0:T(8,128)(2,1)S(1)}, f32[4,2,256]{2,1,0:T(2,128)S(1)}, bf16[4,256,256]{2,1,0:T(8,128)(2,1)S(1)}, /*index=5*/s32[]{:T(128)}, s32[]{:T(128)}) while((s32[]{:T(128)}, f32[256,2,256]{2,0,1:T(8,128)}, bf16[4,256,256]{2,1,0:T(8,128)(2,1)S(1)}, ...), condition=%wide.region_10.11_spmd.clone, body=%wide.region_9.10_spmd.clone.sunk | while | flops 67698688 | bytes 1841251 | solution.py:169
  179.0 2.1 convolution_add_fusion.9
  181.1 2.1 convolution_add_fusion.9
  183.2 2.1 convolution_add_fusion.9
  185.4 25.1 %reduce-scatter.7.cloned.1.call-done = f32[32,2,256]{2,0,1:T(8,128)} async-done(((f32[256,2,256]{2,0,1:T(8,128)}), f32[32,2,256]{2,0,1:T(8,128)}) %reduce-scatter.7.cloned.1.call-update) | async-done | bytes 65552 | tf_op jit(solution)/shard_map/reduce_scatter | solution.py:214
  212.4 14.3 %all_to_all.136 = f32[8,1,2048]{2,1,0:T(1,128)S(1)} all-to-all(f32[8,1,2048]{2,1,0:T(1,128)S(1)} %reshape.884), channel_id=1, replica_groups=mesh['grp'=2,'tile'=4,'coil'=2,'spk'=2] {'tile','spk'}, dimensions={0} | all-to-all | bytes 131072 | tf_op jit(solution)/shard_map/all_to_all | solution.py:221
  229.4 19.1 %all-reduce.8.cloned.1.call-done = f32[32,2,256]{2,0,1:T(8,128)} async-done(((f32[32,2,256]{2,0,1:T(8,128)}), f32[32,2,256]{2,0,1:T(8,128)}) %all-reduce.8.cloned.1.call-update) | async-done | bytes 65552 | tf_op jit(solution)/shard_map/psum | solution.py:225
  254.0 1.9 reshape.886
  255.9 5.9 %all-to-all-start.5 = ((f32[8,1,2048]{2,1,0:T(1,128)}), f32[8,1,2048]{2,1,0:T(1,128)}, u32[]{:S(2)}, u32[]{:S(2)}) async-start(f32[8,1,2048]{2,1,0:T(1,128)} %reshape.886), calls=%async_computation.7 | async-start | bytes 131072 | tf_op jit(solution)/shard_map/all_to_all | solution.py:182
  261.8 4.4 all-to-all-done.5
  266.1 2.2 reduce.3
  268.4 1.8 reshape.887
  270.2 1.8 copy.226
  272.0 1.7 reshape.857
  275.2 13.2 %all_gather.14 = bf16[256,2,256]{2,0,1:T(8,128)(2,1)S(1)} all-gather(bf16[32,2,256]{2,0,1:T(8,128)(2,1)S(1)} %fusion.33), channel_id=1, replica_groups=mesh['grp'=2,'tile'=4,'coil'=2,'spk'=2] {'tile','spk'}, dimensions={0}, use_global_device_ids=true | all-gather | bytes 294912 | tf_op jit(solution)/shard_map/all_gather | solution.py:188
  289.4 12.7 %while.96 = (s32[]{:T(128)}, f32[4,2,256]{2,1,0:T(2,128)}, bf16[4,256,256]{2,1,0:T(8,128)(2,1)S(1)}, bf16[512,256]{1,0:T(8,128)(2,1)S(1)}, bf16[4,256,256]{2,1,0:T(8,128)(2,1)S(1)}, /*index=5*/s32[]{:T(128)}) while((s32[]{:T(128)}, f32[4,2,256]{2,1,0:T(2,128)}, bf16[4,256,256]{2,1,0:T(8,128)(2,1)S(1)}, bf16[512,256]{1,0:T(8,128)(2,1)S(1)}, ...), condition=%wide.region_15.16_spmd, body=%wide.region_13.15_spmd.sunk | while | flops 67436544 | bytes 6300293 | solution.py:209
  303.5 7.5 %while.100 = (s32[]{:T(128)}, f32[256,2,256]{2,0,1:T(8,128)}, bf16[4,256,256]{2,1,0:T(8,128)(2,1)S(1)}, f32[4,2,256]{2,1,0:T(2,128)S(1)}, bf16[4,256,256]{2,1,0:T(8,128)(2,1)S(1)}, /*index=5*/s32[]{:T(128)}, s32[]{:T(128)}) while((s32[]{:T(128)}, f32[256,2,256]{2,0,1:T(8,128)}, bf16[4,256,256]{2,1,0:T(8,128)(2,1)S(1)}, ...), condition=%wide.region_17.18_spmd.clone, body=%wide.region_16.17_spmd.clone.sunk | while | flops 67698688 | bytes 1841251 | solution.py:169
  304.6 2.1 convolution_add_fusion.10
  306.8 2.1 convolution_add_fusion.10
  308.9 2.1 convolution_add_fusion.10
  311.3 25.0 %reduce-scatter.9.cloned.1.call-done = f32[32,2,256]{2,0,1:T(8,128)} async-done(((f32[256,2,256]{2,0,1:T(8,128)}), f32[32,2,256]{2,0,1:T(8,128)}) %reduce-scatter.9.cloned.1.call-update) | async-done | bytes 65552 | tf_op jit(solution)/shard_map/reduce_scatter | solution.py:214
  338.2 14.0 %all_to_all.137 = f32[8,1,2048]{2,1,0:T(1,128)S(1)} all-to-all(f32[8,1,2048]{2,1,0:T(1,128)S(1)} %reshape.888), channel_id=1, replica_groups=mesh['grp'=2,'tile'=4,'coil'=2,'spk'=2] {'tile','spk'}, dimensions={0} | all-to-all | bytes 131072 | tf_op jit(solution)/shard_map/all_to_all | solution.py:221
  355.0 19.0 %all-reduce.10.cloned.1.call-done = f32[32,2,256]{2,0,1:T(8,128)} async-done(((f32[32,2,256]{2,0,1:T(8,128)}), f32[32,2,256]{2,0,1:T(8,128)}) %all-reduce.10.cloned.1.call-update) | async-done | bytes 65552 | tf_op jit(solution)/shard_map/psum | solution.py:225
  379.5 1.9 reshape.890
  381.4 5.9 %all-to-all-start.7 = ((f32[8,1,2048]{2,1,0:T(1,128)}), f32[8,1,2048]{2,1,0:T(1,128)}, u32[]{:S(2)}, u32[]{:S(2)}) async-start(f32[8,1,2048]{2,1,0:T(1,128)} %reshape.890), calls=%async_computation.10 | async-start | bytes 131072 | tf_op jit(solution)/shard_map/all_to_all | solution.py:182
  387.3 4.4 all-to-all-done.7
  391.6 2.2 reduce.5
  393.9 1.8 reshape.891
  395.7 1.8 copy.224
  397.5 1.7 reshape.866
  400.7 13.1 %all_gather.15 = bf16[256,2,256]{2,0,1:T(8,128)(2,1)S(1)} all-gather(bf16[32,2,256]{2,0,1:T(8,128)(2,1)S(1)} %fusion.34), channel_id=1, replica_groups=mesh['grp'=2,'tile'=4,'coil'=2,'spk'=2] {'tile','spk'}, dimensions={0}, use_global_device_ids=true | all-gather | bytes 294912 | tf_op jit(solution)/shard_map/all_gather | solution.py:188
  414.9 12.7 %while.97 = (s32[]{:T(128)}, f32[4,2,256]{2,1,0:T(2,128)}, bf16[4,256,256]{2,1,0:T(8,128)(2,1)S(1)}, bf16[512,256]{1,0:T(8,128)(2,1)S(1)}, bf16[4,256,256]{2,1,0:T(8,128)(2,1)S(1)}, /*index=5*/s32[]{:T(128)}) while((s32[]{:T(128)}, f32[4,2,256]{2,1,0:T(2,128)}, bf16[4,256,256]{2,1,0:T(8,128)(2,1)S(1)}, bf16[512,256]{1,0:T(8,128)(2,1)S(1)}, ...), condition=%wide.region_22.23_spmd, body=%wide.region_20.22_spmd.sunk | while | flops 67436544 | bytes 6300293 | solution.py:209
  429.0 7.5 %while.101 = (s32[]{:T(128)}, f32[256,2,256]{2,0,1:T(8,128)}, bf16[4,256,256]{2,1,0:T(8,128)(2,1)S(1)}, f32[4,2,256]{2,1,0:T(2,128)S(1)}, bf16[4,256,256]{2,1,0:T(8,128)(2,1)S(1)}, /*index=5*/s32[]{:T(128)}, s32[]{:T(128)}) while((s32[]{:T(128)}, f32[256,2,256]{2,0,1:T(8,128)}, bf16[4,256,256]{2,1,0:T(8,128)(2,1)S(1)}, ...), condition=%wide.region_24.25_spmd.clone, body=%wide.region_23.24_spmd.clone.sunk | while | flops 67698688 | bytes 1841251 | solution.py:169
  430.2 2.1 convolution_add_fusion.11
  432.3 2.1 convolution_add_fusion.11
  434.4 2.1 convolution_add_fusion.11
  436.6 25.3 %reduce-scatter.11.cloned.1.call-done = f32[32,2,256]{2,0,1:T(8,128)} async-done(((f32[256,2,256]{2,0,1:T(8,128)}), f32[32,2,256]{2,0,1:T(8,128)}) %reduce-scatter.11.cloned.1.call-update) | async-done | bytes 65552 | tf_op jit(solution)/shard_map/reduce_scatter | solution.py:214
  463.9 13.9 %all_to_all.138 = f32[8,1,2048]{2,1,0:T(1,128)S(1)} all-to-all(f32[8,1,2048]{2,1,0:T(1,128)S(1)} %reshape.892), channel_id=1, replica_groups=mesh['grp'=2,'tile'=4,'coil'=2,'spk'=2] {'tile','spk'}, dimensions={0} | all-to-all | bytes 131072 | tf_op jit(solution)/shard_map/all_to_all | solution.py:221
  480.6 19.0 %all-reduce.12.cloned.1.call-done = f32[32,2,256]{2,0,1:T(8,128)} async-done(((f32[32,2,256]{2,0,1:T(8,128)}), f32[32,2,256]{2,0,1:T(8,128)}) %all-reduce.12.cloned.1.call-update) | async-done | bytes 65552 | tf_op jit(solution)/shard_map/psum | solution.py:225
  (390 shorter events, 116.7 us)
Async XLA Ops:
  6.5 10.6 %copy-start = (s32[8,256]{1,0:T(8,128)S(1)}, s32[8,256]{1,0:T(8,128)}, u32[]{:S(2)}) copy-start(s32[8,256]{1,0:T(8,128)} %param.23) | copy-start | bytes 24580
  18.3 15.0 %all-to-all-start = ((s32[8,1,256]{2,1,0:T(1,128)}), s32[8,1,256]{2,1,0:T(1,128)S(1)}, u32[]{:S(2)}, u32[]{:S(2)}) async-start(s32[8,1,256]{2,1,0:T(1,128)} %copy.115), calls=%async_computation | async-start | bytes 16384 | tf_op jit(solution)/shard_map/all_to_all | solution.py:135
  27.0 30.2 %copy-start.26 = (s32[8]{0:T(128)}, s32[8]{0:T(128)S(1)}, u32[]{:S(2)}) copy-start(s32[8]{0:T(128)S(1)} %get-tuple-element.881) | copy-start | bytes 100
  27.0 30.2 %copy-start.28 = (s32[8]{0:T(128)}, s32[8]{0:T(128)S(1)}, u32[]{:S(2)}) copy-start(s32[8]{0:T(128)S(1)} %get-tuple-element.882) | copy-start | bytes 100
  28.1 0.7 copy-start.19
  28.8 1.3 copy-start.23
  30.3 117.7 %copy-start.1 = (f32[1,256,2,256]{3,1,2,0:T(8,128)}, f32[1,256,2,256]{3,1,2,0:T(8,128)S(1)}, u32[]{:S(2)}) copy-start(f32[1,256,2,256]{3,1,2,0:T(8,128)S(1)} %get-tuple-element.830) | copy-start | bytes 1572868
  30.3 117.7 %copy-start.4 = (f32[1,256,2,256]{3,1,2,0:T(8,128)}, f32[1,256,2,256]{3,1,2,0:T(8,128)S(1)}, u32[]{:S(2)}) copy-start(f32[1,256,2,256]{3,1,2,0:T(8,128)S(1)} %get-tuple-element.833) | copy-start | bytes 1572868
  33.3 9.2 %all-to-all-start.1 = ((bf16[8,1,8,256]{3,2,1,0:T(8,128)(2,1)}), bf16[8,1,8,256]{3,2,1,0:T(8,128)(2,1)S(1)}, u32[]{:S(2)}, u32[]{:S(2)}) async-start(bf16[8,1,8,256]{3,2,1,0:T(8,128)(2,1)} %bitcast.26), calls=%async_computation.1 | async-start | bytes 65536 | tf_op jit(solution)/shard_map/all_to_all | solution.py:132
  38.4 38.2 %reduce-scatter.5.cloned.1.call-start = ((), (), s32[]{:S(2)}) async-start(), calls=%async_computation.13 | async-start | bytes 589824 | tf_op jit(solution)/shard_map/reduce_scatter | solution.py:214
  80.9 15.2 %all-to-all-start.2 = ((f32[8,1,2048]{2,1,0:T(1,128)}), f32[8,1,2048]{2,1,0:T(1,128)S(1)}, u32[]{:S(2)}, u32[]{:S(2)}) async-start(f32[8,1,2048]{2,1,0:T(1,128)} %reshape.880), calls=%async_computation.3 | async-start | bytes 131072 | tf_op jit(solution)/shard_map/all_to_all | solution.py:221
  91.8 31.2 %all-reduce.6.cloned.1.call-start = ((), (), s32[]{:S(2)}) async-start(), calls=%async_computation.14 | async-start | bytes 131072 | tf_op jit(solution)/shard_map/psum | solution.py:225
  103.5 0.7 copy-start.31
  104.2 0.7 copy-start.32
  104.2 0.7 copy-start.33
  104.2 0.7 copy-start.34
  104.2 0.7 copy-start.35
  104.2 0.7 copy-start.27
  104.2 0.7 copy-start.29
  104.2 0.7 copy-start.30
  124.1 0.7 copy-start.14
  130.2 10.2 %all-to-all-start.3 = ((f32[8,1,2048]{2,1,0:T(1,128)}), f32[8,1,2048]{2,1,0:T(1,128)}, u32[]{:S(2)}, u32[]{:S(2)}) async-start(f32[8,1,2048]{2,1,0:T(1,128)} %reshape.882), calls=%async_computation.4 | async-start | bytes 131072 | tf_op jit(solution)/shard_map/all_to_all | solution.py:182
  136.1 74.3 %reduce-scatter.7.cloned.1.call-start = ((), (), s32[]{:S(2)}) async-start(), calls=%async_computation.15 | async-start | bytes 589824 | tf_op jit(solution)/shard_map/reduce_scatter | solution.py:214
  163.7 0.7 copy-start.9
  165.2 1.6 copy-start.10
  166.9 0.7 copy-start.9
  168.4 1.6 copy-start.10
  170.1 0.7 copy-start.9
  171.6 1.6 copy-start.10
  173.2 0.7 copy-start.9
  174.8 1.6 copy-start.10
  176.4 0.7 copy-start.20
  185.3 63.2 %all-reduce.8.cloned.1.call-start = ((), (), s32[]{:S(2)}) async-start(), calls=%async_computation.16 | async-start | bytes 131072 | tf_op jit(solution)/shard_map/psum | solution.py:225
  248.5 1.4 copy-start.15
  249.6 1.0 copy-start.5
  249.9 1.1 copy-start.2
  255.9 10.2 %all-to-all-start.5 = ((f32[8,1,2048]{2,1,0:T(1,128)}), f32[8,1,2048]{2,1,0:T(1,128)}, u32[]{:S(2)}, u32[]{:S(2)}) async-start(f32[8,1,2048]{2,1,0:T(1,128)} %reshape.886), calls=%async_computation.7 | async-start | bytes 131072 | tf_op jit(solution)/shard_map/all_to_all | solution.py:182
  261.8 74.5 %reduce-scatter.9.cloned.1.call-start = ((), (), s32[]{:S(2)}) async-start(), calls=%async_computation.17 | async-start | bytes 589824 | tf_op jit(solution)/shard_map/reduce_scatter | solution.py:214
  289.4 0.7 copy-start.11
  290.9 1.6 copy-start.12
  292.6 0.7 copy-start.11
  294.1 1.6 copy-start.12
  295.7 0.7 copy-start.11
  297.3 1.6 copy-start.12
  298.9 0.7 copy-start.11
  300.4 1.6 copy-start.12
  302.1 0.7 copy-start.21
  311.0 63.0 %all-reduce.10.cloned.1.call-start = ((), (), s32[]{:S(2)}) async-start(), calls=%async_computation.18 | async-start | bytes 131072 | tf_op jit(solution)/shard_map/psum | solution.py:225
  374.0 1.4 copy-start.16
  375.1 1.0 copy-start.6
  375.4 1.1 copy-start.3
  381.4 10.2 %all-to-all-start.7 = ((f32[8,1,2048]{2,1,0:T(1,128)}), f32[8,1,2048]{2,1,0:T(1,128)}, u32[]{:S(2)}, u32[]{:S(2)}) async-start(f32[8,1,2048]{2,1,0:T(1,128)} %reshape.890), calls=%async_computation.10 | async-start | bytes 131072 | tf_op jit(solution)/shard_map/all_to_all | solution.py:182
  387.3 74.6 %reduce-scatter.11.cloned.1.call-start = ((), (), s32[]{:S(2)}) async-start(), calls=%async_computation.19 | async-start | bytes 589824 | tf_op jit(solution)/shard_map/reduce_scatter | solution.py:214
  414.9 0.7 copy-start.7
  416.4 1.6 copy-start.8
  418.1 0.7 copy-start.7
  419.6 1.6 copy-start.8
  421.2 0.7 copy-start.7
  422.8 1.6 copy-start.8
  424.4 0.7 copy-start.7
  426.0 1.6 copy-start.8
  427.6 0.7 copy-start.22
  436.5 63.0 %all-reduce.12.cloned.1.call-start = ((), (), s32[]{:S(2)}) async-start(), calls=%async_computation.20 | async-start | bytes 131072 | tf_op jit(solution)/shard_map/psum | solution.py:225
  500.6 0.7 copy-start.17
  (4 other events, 2.5 us)
Sparse Core Ops, SparseCore 0:
  52.9 23.6 reduce-scatter.4
  104.3 18.6 all-reduce.5
  185.4 24.9 reduce-scatter.6
  229.6 18.8 all-reduce.7
  311.1 25.0 reduce-scatter.8
  355.1 18.8 all-reduce.9
  436.7 25.2 reduce-scatter.10
  480.7 18.8 all-reduce.11
where the time goes:
time: 516 us; the launch traced here: 509 us
  waiting for transfers between devices  187 us (36%)
  blocking collectives  88.2 us (17%)
  local copies, waits for them, and re-layouts  69.4 us (13%)
  matrix products  62 us (12%)
  other arithmetic  46.1 us (9%)
  starting transfers between devices  40.7 us (8%)
  between operations  15 us (3%)
    reduce_scatter x4, waiting for transfers between devices, local(): lax.psum_scatter(grid_term(jnp.int32(0), row_count * lax.axis_size(('tile...  93.9 us
    psum x4, waiting for transfers between devices, local(): gradient = lax.psum(conj_mul(coil_sens, coil_back), 'coil')  75.1 us
    all_to_all x3, blocking collectives, local(): lax.all_to_all(partial_back, ('tile', 'spk'), split_axis=2, concat_axis=0...  42.3 us
    all_gather x3, blocking collectives, local(): piece = lax.all_gather(kspace, ('tile', 'spk'), axis=0, tiled=True)  39.4 us
    dot_general x16, matrix products, grid_one_spoke(): jnp.dot(smeared.reshape(piece_rows * 2, RO), row_one, preferred_element_t...  29.1 us
    unnamed x82, local copies, waits for them, and re-layouts  24.4 us
    all_to_all x3, starting transfers between devices, local(): lax.all_to_all(half_done, ('tile', 'spk'), split_axis=2, concat_axis=0, t...  17.6 us
    dynamic_update_slice x12, other arithmetic, fold_one_spoke(): lax.dynamic_update_index_in_dim(partial_value, current + added, spoke_ind...  15.1 us
  transfers between devices with their start and end apart: 14, of which 13 were waited for; matrix products, arithmetic and copies ran while one was open for 3% of the time, Pallas kernels for 0%

commit v1 on v0

v1 whole, which is shorter than its diff:
```python
import functools
import math

import jax
import jax.numpy as jnp
import numpy as np
from jax import lax
from jax.experimental import pallas as pl
from jax.experimental.pallas import tpu as pltpu
from jax.sharding import PartitionSpec as P

SPK_DEV = 8
LEVELS = 3
ITERS = 4
CORES = 2
CHUNKS = 4
GROUP = 4
STEP_SIZE = 0.5
LANES = 128
F32 = jnp.float32
BF16 = jnp.bfloat16
MESH = pl.DeviceIdType.MESH


def split_np(table):
    high = table.astype(jnp.bfloat16)
    low = (table - high.astype(np.float32)).astype(jnp.bfloat16)
    return high, low


def haar_signs(length, levels):
    mat = np.eye(length)
    for level in range(levels):
        span = length >> level
        half = span // 2
        step = np.eye(length)
        step[:span] = 0.0
        for i in range(half):
            step[i, 2 * i] = step[i, 2 * i + 1] = 1.0
            step[half + i, 2 * i] = 1.0
            step[half + i, 2 * i + 1] = -1.0
        mat = step @ mat
    return mat


def haar_labels(length, levels):
    label = np.ones((length,), np.int32)
    for level in range(1, levels + 1):
        label = label + (np.arange(length) < length >> level)
    return label


def tables(n, levels, chunk):
    phase = np.outer(np.arange(n), np.arange(n)) % n
    angle = phase * (2.0 * np.pi / n)
    cosine = (np.cos(angle) / math.sqrt(n)).astype(np.float32)
    sine = (np.sin(angle) / math.sqrt(n)).astype(np.float32)
    wide = np.concatenate([cosine, sine], axis=1)
    tall = np.concatenate([cosine, sine], axis=0)
    col = haar_signs(n, levels)
    block = 2**levels
    small = haar_signs(block, levels)
    rows = np.kron(np.eye(chunk // block), small)
    col_norm = 1.0 / np.sqrt((col**2).sum(1))
    row_norm = 1.0 / np.sqrt((small**2).sum(1))
    scale = np.tile(row_norm[:, None] * col_norm[None, :], (chunk // block, 1))
    label = np.minimum(haar_labels(block, levels)[:, None], haar_labels(n, levels)[None, :])
    label = np.tile(label, (chunk // block, 1))
    wide_h, wide_l = split_np(wide)
    tall_h, tall_l = split_np(tall)
    as_bf = lambda a: np.ascontiguousarray(a).astype(jnp.bfloat16)
    return (
        wide_h, wide_l, tall_h, tall_l,
        as_bf(col.T), as_bf(col), as_bf(rows), as_bf(rows.T),
        scale.astype(np.float32), label.astype(np.int32),
    )


def split(x):
    high = x.astype(BF16)
    return high, (x - high.astype(F32)).astype(BF16)


def mm(a, b):
    return jnp.dot(a, b, preferred_element_type=F32)


def mm3(a, b):
    return mm(a[0], b[0]) + (mm(a[0], b[1]) + mm(a[1], b[0]))


def kernel(
    dims,
    thr_ref, meta_ref, data_ref, map_ref,
    wide_h, wide_l, tall_h, tall_l, col_t, col_m, row_m, row_t, scale_ref, label_ref,
    out_ref,
    meta_all, data_all, maps, comp, comp_data, row_tab, col_tab, kspace, grid, back_h, back_l,
    half_h, half_l, estimate, grads,
    meta_send, meta_recv, data_send, data_recv, map_send, map_recv, grad_send, grad_recv,
):
    n, tiles, coils, rows, live = dims
    blocks = tiles * CORES
    chunk = n // CHUNKS
    coil, tile, core = lax.axis_index("coil"), lax.axis_index("tile"), lax.axis_index("spk")
    pair, bit = coil // CORES, coil % CORES
    block = tile * CORES + core
    mine = pair * CORES + core

    sends = []
    for d_tile in range(tiles):
        for d_core in range(CORES):
            if d_tile == 0 and d_core == 0:
                continue
            copy = pltpu.make_async_remote_copy(
                src_ref=meta_ref,
                dst_ref=meta_all.at[block],
                send_sem=meta_send.at[d_tile * CORES + d_core],
                recv_sem=meta_recv.at[block],
                device_id={"tile": (tile + d_tile) % tiles, "spk": (core + d_core) % CORES},
                device_id_type=MESH,
            )
            copy.start()
            sends.append(copy)
    for src, dst, s_sem, r_sem in (
        (data_ref, data_all.at[block], data_send, data_recv),
        (map_ref, maps.at[:, block], map_send, map_recv),
    ):
        for d_bit in range(CORES):
            for d_tile in range(tiles):
                copy = pltpu.make_async_remote_copy(
                    src_ref=src,
                    dst_ref=dst,
                    send_sem=s_sem.at[d_bit * tiles + d_tile],
                    recv_sem=r_sem.at[block],
                    device_id={
                        "coil": pair * CORES + (bit + d_bit) % CORES,
                        "tile": (tile + d_tile) % tiles,
                        "spk": bit,
                    },
                    device_id_type=MESH,
                )
                if d_bit == 0 and d_tile == 0:
                    local_copy = pltpu.make_async_copy(src, dst, r_sem.at[block])

                    @pl.when(core == bit)
                    def _(local_copy=local_copy):
                        local_copy.start()

                    @pl.when(core != bit)
                    def _(copy=copy):
                        copy.start()
                        copy.wait_send()
                else:
                    copy.start()
                    sends.append(copy)

    meta_all[block] = meta_ref[...]
    for d_block in range(1, blocks):
        other = (block + d_block) % blocks
        pltpu.make_async_copy(meta_all.at[other], meta_all.at[other], meta_recv.at[other]).wait()

    slots = blocks * SPK_DEV * 2
    packed = meta_all[...].reshape(slots, meta_ref.shape[1])
    up = lax.broadcasted_iota(jnp.int32, (slots, slots), 0) // 2
    across = lax.broadcasted_iota(jnp.int32, (slots, slots), 1) // 2
    parity = lax.broadcasted_iota(jnp.int32, (slots, LANES), 0) % 2
    flag = jnp.where((packed[:, :LANES].astype(F32) >= 0.0) & (parity == 0), 1.0 / LANES, 0.0)
    flags = lax.dot_general(
        jnp.ones((LANES, LANES), BF16), flag.astype(BF16), (((1,), (1,)), ((), ())),
        preferred_element_type=F32,
    ).astype(BF16)
    rank = mm(flags, jnp.where(up < across, 1.0, 0.0).astype(BF16))
    alive = mm(flags, jnp.where(up == across, 1.0, 0.0).astype(BF16))
    place = lax.broadcasted_iota(jnp.int32, (LANES, slots), 0)
    which = lax.broadcasted_iota(jnp.int32, (LANES, slots), 1) % 2
    hit = (alive > 0.5) & (rank.astype(jnp.int32) == place)
    pick = [jnp.where(hit & (which == h), 1.0, 0.0).astype(BF16) for h in range(2)]
    for h in range(2):
        comp[h] = mm(pick[h], packed)

    cells = lax.broadcasted_iota(jnp.int32, (n, n), 0)

    def build(i, carry):
        def table(centre, weights):
            gap = (cells - centre.astype(jnp.int32) + 1) & (n - 1)
            return jnp.where(
                gap == 0, weights[0], jnp.where(gap == 1, weights[1], jnp.where(gap == 2, weights[2], 0.0))
            ).astype(BF16)

        def part(h, j):
            return comp[h, pl.ds(i, 1), j * n : (j + 1) * n]

        row_tab[i] = table(part(0, 0), (part(0, 2), part(0, 3), part(1, 0)))
        col_tab[i] = table(part(0, 1), (part(1, 1), part(1, 2), part(1, 3)))
        return carry

    lax.fori_loop(0, live, build, 0)

    for b in range(blocks):
        pltpu.make_async_copy(data_all.at[b], data_all.at[b], data_recv.at[b]).wait()
    samples = data_all[...].reshape(slots, n)
    for h in range(2):
        comp_data[h] = mm(pick[h], samples)

    offset = jnp.abs(lax.broadcasted_iota(jnp.int32, (1, n), 1) - n // 2).astype(F32)
    density = (offset + 0.5) * (n / (3.0 * n * live))
    wide = (wide_h[...], wide_l[...])
    tall = (tall_h[...], tall_l[...])

    for it in range(ITERS):
        slot = it % 2
        grid[...] = jnp.zeros_like(grid)

        def spokes(step, carry, it=it):
            total = None
            for g in range(GROUP):
                i = step * GROUP + g
                real = -comp_data[0, pl.ds(i, 1), :]
                imag = -comp_data[1, pl.ds(i, 1), :]
                col = col_tab[i]
                if it > 0:
                    inner = mm(kspace[...], col)
                    row = row_tab[i].astype(F32)
                    real = real + jnp.sum(inner[:n] * row, axis=0, keepdims=True)
                    imag = imag + jnp.sum(inner[n:] * row, axis=0, keepdims=True)
                real, imag = density * real, density * imag
                wide_col = col.astype(F32)
                smeared = jnp.concatenate(
                    [(wide_col * real).astype(BF16), (wide_col * imag).astype(BF16)], axis=0
                )
                added = lax.dot_general(
                    row_tab[i], smeared, (((1,), (1,)), ((), ())), preferred_element_type=F32
                )
                total = added if total is None else total + added
            grid[...] += total
            return carry

        lax.fori_loop(0, live // GROUP, spokes, 0)

        turned = mm3(tall, split(grid[...]))
        for p, value in enumerate(
            (turned[:n, :n] - turned[n:, n:], turned[:n, n:] + turned[n:, :n])
        ):
            back_h[p], back_l[p] = split(value)
        if it == 0:
            for b in range(blocks):
                pltpu.make_async_copy(maps.at[:, b], maps.at[:, b], map_recv.at[b]).wait()

        def sens(q):
            whole = maps.at[:, pl.ds(q * (blocks // CHUNKS), blocks // CHUNKS)][...]
            whole = whole.reshape(2, chunk, n)
            return whole[0], whole[1]

        copies = []
        for q in range(CHUNKS):
            rs = slice(q * chunk, (q + 1) * chunk)
            b_h = back_h[:, rs, :].reshape(2 * chunk, n)
            b_l = back_l[:, rs, :].reshape(2 * chunk, n)
            image = mm3((b_h, b_l), wide)
            d_r = image[:chunk, :n] - image[chunk:, n:]
            d_i = image[:chunk, n:] + image[chunk:, :n]
            m_r, m_i = sens(q)
            grads[slot, q, mine, 0] = m_r * d_r + m_i * d_i
            grads[slot, q, mine, 1] = m_r * d_i - m_i * d_r
            for d in range(1, coils):
                d_pair, d_core = d // CORES, d % CORES
                copy = pltpu.make_async_remote_copy(
                    src_ref=grads.at[slot, q, mine],
                    dst_ref=grads.at[slot, q, mine],
                    send_sem=grad_send.at[slot, q, d],
                    recv_sem=grad_recv.at[slot, q, mine],
                    device_id={
                        "coil": (coil + d_pair * CORES) % coils,
                        "spk": (core + d_core) % CORES,
                    },
                    device_id_type=MESH,
                )
                copy.start()
                copies.append(copy)

        limits = jnp.ones((chunk, n), F32)
        label = label_ref[...]
        for level in range(LEVELS):
            limits = jnp.where(label == level + 1, thr_ref[level], limits)
        active = label <= LEVELS
        scale = scale_ref[...]
        for q in range(CHUNKS):
            for d in range(1, coils):
                d_pair, d_core = d // CORES, d % CORES
                other = (coil + d_pair * CORES) % coils // CORES * CORES + (core + d_core) % CORES
                pltpu.make_async_copy(
                    grads.at[slot, q, other], grads.at[slot, q, other], grad_recv.at[slot, q, other]
                ).wait()
            summed = grads[slot, q, 0]
            for c in range(1, coils):
                summed = summed + grads[slot, q, c]
            rs = slice(q * chunk, (q + 1) * chunk)
            target = -STEP_SIZE * summed
            if it > 0:
                target = estimate[:, rs, :] + target
            t_h, t_l = split(target.reshape(2 * chunk, n))
            along = mm(t_h, col_t[...]) + mm(t_l, col_t[...])
            side = split(jnp.concatenate([along[:chunk], along[chunk:]], axis=1))
            coeffs = mm(row_m[...], side[0]) + mm(row_m[...], side[1])
            c_r, c_i = coeffs[:, :n] * scale, coeffs[:, n:] * scale
            size = jnp.sqrt(c_r * c_r + c_i * c_i)
            factor = jnp.maximum(size - limits, 0.0) / jnp.maximum(size, limits)
            factor = jnp.where(active, factor, 1.0) * scale
            side = split(jnp.concatenate([c_r * factor, c_i * factor], axis=1))
            along = mm(row_t[...], side[0]) + mm(row_t[...], side[1])
            t_h, t_l = split(jnp.concatenate([along[:, :n], along[:, n:]], axis=0))
            fresh = mm(t_h, col_m[...]) + mm(t_l, col_m[...])
            e_r, e_i = fresh[:chunk], fresh[chunk:]
            estimate[0, rs, :] = e_r
            estimate[1, rs, :] = e_i
            if it < ITERS - 1:
                m_r, m_i = sens(q)
                seen = split(
                    jnp.concatenate([m_r * e_r - m_i * e_i, m_r * e_i + m_i * e_r], axis=0)
                )
                w = mm3(seen, wide)
                half = jnp.concatenate(
                    [w[:chunk, :n] + w[chunk:, n:], w[chunk:, :n] - w[:chunk, n:]], axis=1
                )
                half_h[rs, :], half_l[rs, :] = split(half)
        for copy in copies:
            copy.wait_send()
        if it < ITERS - 1:
            v = mm3(tall, (half_h[...], half_l[...]))
            kspace[:n, :] = (v[:n, :n] + v[n:, n:]).astype(BF16)
            kspace[n:, :] = (v[:n, n:] - v[n:, :n]).astype(BF16)

    out_ref[...] = estimate[:, pl.ds(pl.multiple_of(block * rows, rows), rows), :]
    for copy in sends:
        copy.wait_send()


def local(coil_maps, kspace_data, interp_weights, sample_bins, spoke_count, thresholds):
    tiles, coils = lax.axis_size("tile"), lax.axis_size("coil")
    blocks = tiles * CORES
    rows, n = coil_maps.shape[1], coil_maps.shape[3]
    live = blocks * SPK_DEV // 2
    chunk = n // CHUNKS
    slot_live = jnp.arange(SPK_DEV, dtype=jnp.int32)[:, None] < spoke_count[0]
    row = jnp.where(slot_live, sample_bins // n, -1).astype(BF16)
    col = (sample_bins % n).astype(BF16)
    meta = jnp.concatenate([row[:, None], col[:, None], interp_weights], axis=1)
    meta = meta.reshape(SPK_DEV * 2, 4 * n)
    data = kspace_data[0].reshape(SPK_DEV * 2, n)
    maps = jnp.transpose(coil_maps[0], (1, 0, 2))
    consts = tables(n, LEVELS, chunk)
    vmem = pl.BlockSpec(memory_space=pltpu.VMEM)
    slots = blocks * SPK_DEV * 2
    dma = pltpu.SemaphoreType.DMA
    out = pl.pallas_call(
        functools.partial(kernel, (n, tiles, coils, rows, live)),
        out_shape=jax.ShapeDtypeStruct((2, rows, n), F32),
        in_specs=[pl.BlockSpec(memory_space=pltpu.SMEM)] + [vmem] * (3 + len(consts)),
        out_specs=vmem,
        scratch_shapes=[
            pltpu.VMEM((blocks, SPK_DEV * 2, 4 * n), BF16),
            pltpu.VMEM((blocks, SPK_DEV * 2, n), BF16),
            pltpu.VMEM((2, blocks, rows, n), F32),
            pltpu.VMEM((2, LANES, 4 * n), F32),
            pltpu.VMEM((2, LANES, n), F32),
            pltpu.VMEM((live, n, n), BF16),
            pltpu.VMEM((live, n, n), BF16),
            pltpu.VMEM((2 * n, n), BF16),
            pltpu.VMEM((n, 2 * n), F32),
            pltpu.VMEM((2, n, n), BF16),
            pltpu.VMEM((2, n, n), BF16),
            pltpu.VMEM((n, 2 * n), BF16),
            pltpu.VMEM((n, 2 * n), BF16),
            pltpu.VMEM((2, n, n), F32),
            pltpu.VMEM((2, CHUNKS, coils, 2, chunk, n), F32),
            dma((blocks,)), dma((blocks,)), dma((blocks,)), dma((blocks,)),
            dma((blocks,)), dma((blocks,)),
            dma((2, CHUNKS, coils)), dma((2, CHUNKS, coils)),
        ],
        compiler_params=pltpu.CompilerParams(
            has_side_effects=True, vmem_limit_bytes=60 * 1024 * 1024
        ),
    )(thresholds, meta, data, maps, *consts)
    return jnp.transpose(out, (1, 0, 2))


def solution(mesh):
    placed = (
        P("coil", ("grp", "tile", "spk"), None, None),
        P("coil", ("grp", "tile", "spk"), None, None),
        P(("grp", "tile", "spk"), None, None),
        P(("grp", "tile", "spk"), None),
        P(("grp", "tile", "spk")),
        P(),
    )
    return jax.shard_map(
        local,
        mesh=mesh,
        in_specs=placed,
        out_specs=P(("grp", "tile", "spk"), None, None),
        check_vma=False,
    )
```

time: 516 us -> 98.4 us (0.19); the launches traced: 509 us -> 98 us
  waiting for transfers between devices: 187 us -> 0 us
  Pallas kernels: 0 us -> 92.3 us
  blocking collectives: 88.2 us -> 0 us
  local copies, waits for them, and re-layouts: 69.4 us -> 4.29 us
  matrix products: 62 us -> 0 us
  other arithmetic: 46.1 us -> 0.79 us
  starting transfers between devices: 40.7 us -> 0 us
  between operations: 15 us -> 0.7 us
    reduce_scatter x4 -> x0, waiting for transfers between devices: 93.9 us -> none  [local(): lax.psum_scatter(grid_term(jnp.int32(0), row_count * lax.axis_size(('tile...]
    pallas_call x0 -> x1, Pallas kernels: none -> 92.3 us  [local(): pl.pallas_call(functools.partial(kernel, (n, tiles, coils, rows, live)),...]
    psum x4 -> x0, waiting for transfers between devices: 75.1 us -> none  [local(): gradient = lax.psum(conj_mul(coil_sens, coil_back), 'coil')]
    dot_general x64 -> x0, matrix products: 62 us -> none  [the longest x16 29.1 us: grid_one_spoke(): jnp.dot(smeared.reshape(piece_rows * 2, RO), row_one, preferred_element_t...]
    all_to_all x3 -> x0, blocking collectives: 42.3 us -> none  [local(): lax.all_to_all(partial_back, ('tile', 'spk'), split_axis=2, concat_axis=0...]
    all_to_all x6 -> x0, starting transfers between devices: 40.3 us -> none  [the longest x3 17.6 us: local(): lax.all_to_all(half_done, ('tile', 'spk'), split_axis=2, concat_axis=0, t...]
    all_gather x3 -> x0, blocking collectives: 39.4 us -> none  [local(): piece = lax.all_gather(kspace, ('tile', 'spk'), axis=0, tiled=True)]
    unnamed x82 -> x5, local copies, waits for them, and re-layouts: 24.4 us -> 0.81 us
  transfers between devices with their start and end apart: 14 -> 0, of which waited for: 13 -> 0; matrix products, arithmetic and copies ran while one was open for 3% -> 0% of each run, Pallas kernels for 0% -> 0%
where the time goes in v1:
time: 98.4 us; the launch traced here: 98 us
  Pallas kernels  92.3 us (94%)
  local copies, waits for them, and re-layouts  4.29 us (4%)
    pallas_call x1, Pallas kernels, local(): pl.pallas_call(functools.partial(kernel, (n, tiles, coils, rows, live)),...  92.3 us

profile of v1, /device:TPU:11, one launch (start us, length us, event | category | flops | bytes accessed | tf_op | source)
XLA Modules:
  0.0 98.0 jit_solution(11161334251911649477)
XLA Ops:
  0.0 0.0 copy-start.1
  0.7 0.8 fusion.6
  1.4 1.3 %reshape_squeeze.3.data_ref = bf16[16,256]{1,0:T(8,128)(2,1)} reshape(bf16[1,8,2,256]{3,2,1,0:T(2,128)(2,1)} %param.17) | data formatting | bytes 16384 | tf_op jit(solution)/shard_map/reshape;squeeze | solution.py:349
  2.7 0.0 copy-done.1
  2.8 0.0 copy-start
  2.8 0.6 reshape.8.meta_ref
  3.4 0.2 copy-done
  3.6 0.6 copy.21
  4.2 92.3 %shard_map.154 = f32[2,32,256]{2,1,0:T(8,128)} custom-call(f32[3]{0:T(128)} %thr_ref.1, bf16[16,1024]{1,0:T(8,128)(2,1)} %reshape.8.meta_ref, bf16[16,256]{1,0:T(8,128)(2,1)} %reshape_squeeze.3.data_ref, f32[2,32,256]{2,1,0:T(8,128)} %bitcast.13, bf16[256,512]{1,0:T(8,128)(2,1)} %constant.49.clone.wide_h, bf16[256,512]{1,0:T(8,128)(2,1)} %constant.50.clone.wide_l, ...), custom_call_target="tpu_custom_call" | custom-call | tf_op jit(solution)/shard_map/pallas_call | solution.py:355
  96.5 1.5 %copy.19 = f32[32,2,256]{2,1,0:T(2,128)} copy(f32[32,2,256]{2,0,1:T(8,128)} %bitcast.12) | data formatting | bytes 131072 | tf_op jit(solution)/shard_map/transpose | solution.py:384
  (3 shorter events, 0.0 us)
Async XLA Ops:
  0.0 2.8 %copy-start.1 = (bf16[8,6,256]{2,0,1:T(8,128)(2,1)S(1)}, bf16[8,6,256]{2,0,1:T(8,128)(2,1)}, u32[]{:S(2)}) copy-start(bf16[8,6,256]{2,0,1:T(8,128)(2,1)} %param.18) | copy-start | bytes 73732
  2.8 0.8 copy-start

commit v2 on v1

--- a/solution.py
+++ b/solution.py
@@ -13,7 +13,7 @@
 LEVELS = 3
 ITERS = 4
 CORES = 2
-CHUNKS = 4
+CHUNKS = 2
 GROUP = 4
 STEP_SIZE = 0.5
 LANES = 128
@@ -72,7 +72,7 @@
     return (
         wide_h, wide_l, tall_h, tall_l,
         as_bf(col.T), as_bf(col), as_bf(rows), as_bf(rows.T),
-        scale.astype(np.float32), label.astype(np.int32),
+        np.ascontiguousarray(scale.T).astype(np.float32), np.ascontiguousarray(label.T).astype(np.int32),
     )
 
 
@@ -95,7 +95,7 @@
     wide_h, wide_l, tall_h, tall_l, col_t, col_m, row_m, row_t, scale_ref, label_ref,
     out_ref,
     meta_all, data_all, maps, comp, comp_data, row_tab, col_tab, kspace, grid, back_h, back_l,
-    half_h, half_l, estimate, grads,
+    half_h, half_l, estimate, grads, sens,
     meta_send, meta_recv, data_send, data_recv, map_send, map_recv, grad_send, grad_recv,
 ):
     n, tiles, coils, rows, live = dims
@@ -105,6 +105,37 @@
     pair, bit = coil // CORES, coil % CORES
     block = tile * CORES + core
     mine = pair * CORES + core
+
+    barrier = pltpu.get_barrier_semaphore()
+    peers = [
+        (d_bit, d_tile, d_core)
+        for d_bit in range(CORES)
+        for d_tile in range(tiles)
+        for d_core in range(CORES)
+        if d_bit + d_tile + d_core > 0
+    ]
+    for d_bit, d_tile, d_core in peers:
+        pl.semaphore_signal(
+            barrier,
+            inc=1,
+            device_id={
+                "coil": pair * CORES + (bit + d_bit) % CORES,
+                "tile": (tile + d_tile) % tiles,
+                "spk": (core + d_core) % CORES,
+            },
+            device_id_type=MESH,
+        )
+    for d in range(CORES, coils):
+        pl.semaphore_signal(
+            barrier,
+            inc=1,
+            device_id={
+                "coil": (coil + d // CORES * CORES) % coils,
+                "spk": (core + d % CORES) % CORES,
+            },
+            device_id_type=MESH,
+        )
+    pl.semaphore_wait(barrier, len(peers) + coils - CORES)
 
     sends = []
     for d_tile in range(tiles):
@@ -121,6 +152,7 @@
             )
             copy.start()
             sends.append(copy)
+    across_core = []
     for src, dst, s_sem, r_sem in (
         (data_ref, data_all.at[block], data_send, data_recv),
         (map_ref, maps.at[:, block], map_send, map_recv),
@@ -149,7 +181,8 @@
                     @pl.when(core != bit)
                     def _(copy=copy):
                         copy.start()
-                        copy.wait_send()
+
+                    across_core.append(copy)
                 else:
                     copy.start()
                     sends.append(copy)
@@ -217,19 +250,17 @@
                 i = step * GROUP + g
                 real = -comp_data[0, pl.ds(i, 1), :]
                 imag = -comp_data[1, pl.ds(i, 1), :]
-                col = col_tab[i]
+                col = col_tab[i].astype(F32)
                 if it > 0:
-                    inner = mm(kspace[...], col)
-                    row = row_tab[i].astype(F32)
-                    real = real + jnp.sum(inner[:n] * row, axis=0, keepdims=True)
-                    imag = imag + jnp.sum(inner[n:] * row, axis=0, keepdims=True)
+                    inner = mm(kspace[...], row_tab[i])
+                    real = real + jnp.sum(inner[:n] * col, axis=0, keepdims=True)
+                    imag = imag + jnp.sum(inner[n:] * col, axis=0, keepdims=True)
                 real, imag = density * real, density * imag
-                wide_col = col.astype(F32)
                 smeared = jnp.concatenate(
-                    [(wide_col * real).astype(BF16), (wide_col * imag).astype(BF16)], axis=0
+                    [(col * real).astype(BF16), (col * imag).astype(BF16)], axis=0
                 )
                 added = lax.dot_general(
-                    row_tab[i], smeared, (((1,), (1,)), ((), ())), preferred_element_type=F32
+                    smeared, row_tab[i], (((1,), (1,)), ((), ())), preferred_element_type=F32
                 )
                 total = added if total is None else total + added
             grid[...] += total
@@ -237,7 +268,7 @@
 
         lax.fori_loop(0, live // GROUP, spokes, 0)
 
-        turned = mm3(tall, split(grid[...]))
+        turned = mm3(split(grid[...]), wide)
         for p, value in enumerate(
             (turned[:n, :n] - turned[n:, n:], turned[:n, n:] + turned[n:, :n])
         ):
@@ -246,20 +277,21 @@
             for b in range(blocks):
                 pltpu.make_async_copy(maps.at[:, b], maps.at[:, b], map_recv.at[b]).wait()
 
-        def sens(q):
-            whole = maps.at[:, pl.ds(q * (blocks // CHUNKS), blocks // CHUNKS)][...]
-            whole = whole.reshape(2, chunk, n)
-            return whole[0], whole[1]
+            per_chunk = blocks // CHUNKS
+            for p in range(2):
+                for q in range(CHUNKS):
+                    part = maps[p, q * per_chunk : (q + 1) * per_chunk].reshape(chunk, n)
+                    sens[p, q] = part.T
 
         copies = []
         for q in range(CHUNKS):
             rs = slice(q * chunk, (q + 1) * chunk)
-            b_h = back_h[:, rs, :].reshape(2 * chunk, n)
-            b_l = back_l[:, rs, :].reshape(2 * chunk, n)
-            image = mm3((b_h, b_l), wide)
-            d_r = image[:chunk, :n] - image[chunk:, n:]
-            d_i = image[:chunk, n:] + image[chunk:, :n]
-            m_r, m_i = sens(q)
+            b_h = jnp.concatenate([back_h[0, :, rs], back_h[1, :, rs]], axis=1)
+            b_l = jnp.concatenate([back_l[0, :, rs], back_l[1, :, rs]], axis=1)
+            image = mm3(tall, (b_h, b_l))
+            d_r = image[:n, :chunk] - image[n:, chunk:]
+            d_i = image[:n, chunk:] + image[n:, :chunk]
+            m_r, m_i = sens[0, q], sens[1, q]
             grads[slot, q, mine, 0] = m_r * d_r + m_i * d_i
             grads[slot, q, mine, 1] = m_r * d_i - m_i * d_r
             for d in range(1, coils):
@@ -278,7 +310,7 @@
                 copy.start()
                 copies.append(copy)
 
-        limits = jnp.ones((chunk, n), F32)
+        limits = jnp.ones((n, chunk), F32)
         label = label_ref[...]
         for level in range(LEVELS):
             limits = jnp.where(label == level + 1, thr_ref[level], limits)
@@ -297,40 +329,50 @@
             rs = slice(q * chunk, (q + 1) * chunk)
             target = -STEP_SIZE * summed
             if it > 0:
-                target = estimate[:, rs, :] + target
-            t_h, t_l = split(target.reshape(2 * chunk, n))
-            along = mm(t_h, col_t[...]) + mm(t_l, col_t[...])
-            side = split(jnp.concatenate([along[:chunk], along[chunk:]], axis=1))
-            coeffs = mm(row_m[...], side[0]) + mm(row_m[...], side[1])
-            c_r, c_i = coeffs[:, :n] * scale, coeffs[:, n:] * scale
+                target = estimate[:, q] + target
+            side = split(jnp.concatenate([target[0], target[1]], axis=1))
+            along = mm(col_m[...], side[0]) + mm(col_m[...], side[1])
+            side = split(jnp.concatenate([along[:, :chunk], along[:, chunk:]], axis=0))
+            coeffs = mm(side[0], row_t[...]) + mm(side[1], row_t[...])
+            c_r, c_i = coeffs[:n] * scale, coeffs[n:] * scale
             size = jnp.sqrt(c_r * c_r + c_i * c_i)
             factor = jnp.maximum(size - limits, 0.0) / jnp.maximum(size, limits)
             factor = jnp.where(active, factor, 1.0) * scale
-            side = split(jnp.concatenate([c_r * factor, c_i * factor], axis=1))
-            along = mm(row_t[...], side[0]) + mm(row_t[...], side[1])
-            t_h, t_l = split(jnp.concatenate([along[:, :n], along[:, n:]], axis=0))
-            fresh = mm(t_h, col_m[...]) + mm(t_l, col_m[...])
-            e_r, e_i = fresh[:chunk], fresh[chunk:]
-            estimate[0, rs, :] = e_r
-            estimate[1, rs, :] = e_i
+            side = split(jnp.concatenate([c_r * factor, c_i * factor], axis=0))
+            along = mm(side[0], row_m[...]) + mm(side[1], row_m[...])
+            side = split(jnp.concatenate([along[:n], along[n:]], axis=1))
+            fresh = mm(col_t[...], side[0]) + mm(col_t[...], side[1])
+            e_r, e_i = fresh[:, :chunk], fresh[:, chunk:]
+            estimate[0, q] = e_r
+            estimate[1, q] = e_i
             if it < ITERS - 1:
-                m_r, m_i = sens(q)
+                m_r, m_i = sens[0, q], sens[1, q]
                 seen = split(
-                    jnp.concatenate([m_r * e_r - m_i * e_i, m_r * e_i + m_i * e_r], axis=0)
-                )
-                w = mm3(seen, wide)
+                    jnp.concatenate([m_r * e_r - m_i * e_i, m_r * e_i + m_i * e_r], axis=1)
+                )
+                w = mm3(tall, seen)
                 half = jnp.concatenate(
-                    [w[:chunk, :n] + w[chunk:, n:], w[chunk:, :n] - w[:chunk, n:]], axis=1
-                )
-                half_h[rs, :], half_l[rs, :] = split(half)
+                    [w[:n, :chunk] + w[n:, chunk:], w[:n, chunk:] - w[n:, :chunk]], axis=0
+                )
+                half_h[:, rs], half_l[:, rs] = split(half)
+            else:
+                per_chunk = blocks // CHUNKS
+                maps[0, q * per_chunk : (q + 1) * per_chunk] = e_r.T.reshape(per_chunk, rows, n)
+                maps[1, q * per_chunk : (q + 1) * per_chunk] = e_i.T.reshape(per_chunk, rows, n)
         for copy in copies:
             copy.wait_send()
         if it < ITERS - 1:
-            v = mm3(tall, (half_h[...], half_l[...]))
+            v = mm3((half_h[...], half_l[...]), wide)
             kspace[:n, :] = (v[:n, :n] + v[n:, n:]).astype(BF16)
-            kspace[n:, :] = (v[:n, n:] - v[n:, :n]).astype(BF16)
-
-    out_ref[...] = estimate[:, pl.ds(pl.multiple_of(block * rows, rows), rows), :]
+            kspace[n:, :] = (v[n:, :n] - v[:n, n:]).astype(BF16)
+
+    out_ref[...] = maps[:, block]
+
+    @pl.when(core != bit)
+    def _():
+        for copy in across_core:
+            copy.wait_send()
+
     for copy in sends:
         copy.wait_send()
 
@@ -366,19 +408,20 @@
             pltpu.VMEM((live, n, n), BF16),
             pltpu.VMEM((live, n, n), BF16),
             pltpu.VMEM((2 * n, n), BF16),
-            pltpu.VMEM((n, 2 * n), F32),
+            pltpu.VMEM((2 * n, n), F32),
             pltpu.VMEM((2, n, n), BF16),
             pltpu.VMEM((2, n, n), BF16),
-            pltpu.VMEM((n, 2 * n), BF16),
-            pltpu.VMEM((n, 2 * n), BF16),
-            pltpu.VMEM((2, n, n), F32),
-            pltpu.VMEM((2, CHUNKS, coils, 2, chunk, n), F32),
+            pltpu.VMEM((2 * n, n), BF16),
+            pltpu.VMEM((2 * n, n), BF16),
+            pltpu.VMEM((2, CHUNKS, n, chunk), F32),
+            pltpu.VMEM((2, CHUNKS, coils, 2, n, chunk), F32),
+            pltpu.VMEM((2, CHUNKS, n, chunk), F32),
             dma((blocks,)), dma((blocks,)), dma((blocks,)), dma((blocks,)),
             dma((blocks,)), dma((blocks,)),
             dma((2, CHUNKS, coils)), dma((2, CHUNKS, coils)),
         ],
         compiler_params=pltpu.CompilerParams(
-            has_side_effects=True, vmem_limit_bytes=60 * 1024 * 1024
+            has_side_effects=True, collective_id=0, vmem_limit_bytes=60 * 1024 * 1024
         ),
     )(thresholds, meta, data, maps, *consts)
     return jnp.transpose(out, (1, 0, 2))

time: 98.4 us -> 83 us (0.84)
  Pallas kernels: 92.3 us -> 75.9 us
    pallas_call x1, Pallas kernels: 92.3 us -> 75.9 us  [local(): pl.pallas_call(functools.partial(kernel, (n, tiles, coils, rows, live)),...]
where the time goes in v2:
time: 83 us; the launch traced here: 81.7 us
  Pallas kernels  75.9 us (91%)
  local copies, waits for them, and re-layouts  4.29 us (5%)
    pallas_call x1, Pallas kernels, local(): pl.pallas_call(functools.partial(kernel, (n, tiles, coils, rows, live)),...  75.9 us

profile of v2, /device:TPU:11, one launch (start us, length us, event | category | flops | bytes accessed | tf_op | source)
XLA Modules:
  0.0 81.7 jit_solution(91031028953014552)
XLA Ops:
  0.0 0.0 copy-start.1
  0.7 0.8 fusion.6
  1.4 1.3 %reshape_squeeze.3.data_ref = bf16[16,256]{1,0:T(8,128)(2,1)} reshape(bf16[1,8,2,256]{3,2,1,0:T(2,128)(2,1)} %param.17) | data formatting | bytes 16384 | tf_op jit(solution)/shard_map/reshape;squeeze | solution.py:391
  2.7 0.0 copy-done.1
  2.8 0.0 copy-start
  2.8 0.6 reshape.8.meta_ref
  3.4 0.2 copy-done
  3.6 0.6 copy.21
  4.2 75.9 %shard_map.154 = f32[2,32,256]{2,1,0:T(8,128)} custom-call(f32[3]{0:T(128)} %thr_ref.1, bf16[16,1024]{1,0:T(8,128)(2,1)} %reshape.8.meta_ref, bf16[16,256]{1,0:T(8,128)(2,1)} %reshape_squeeze.3.data_ref, f32[2,32,256]{2,1,0:T(8,128)} %bitcast.13, bf16[256,512]{1,0:T(8,128)(2,1)} %constant.49.clone.wide_h, bf16[256,512]{1,0:T(8,128)(2,1)} %constant.50.clone.wide_l, ...), custom_call_target="tpu_custom_call" | custom-call | tf_op jit(solution)/shard_map/pallas_call | solution.py:397
  80.1 1.5 %copy.19 = f32[32,2,256]{2,1,0:T(2,128)} copy(f32[32,2,256]{2,0,1:T(8,128)} %bitcast.12) | data formatting | bytes 131072 | tf_op jit(solution)/shard_map/transpose | solution.py:427
  (3 shorter events, 0.0 us)
Async XLA Ops:
  0.0 2.8 %copy-start.1 = (bf16[8,6,256]{2,0,1:T(8,128)(2,1)S(1)}, bf16[8,6,256]{2,0,1:T(8,128)(2,1)}, u32[]{:S(2)}) copy-start(bf16[8,6,256]{2,0,1:T(8,128)(2,1)} %param.18) | copy-start | bytes 73732
  2.8 0.8 %copy-start = (f32[1,32,2,256]{3,2,1,0:T(2,128)S(1)}, f32[1,32,2,256]{3,2,1,0:T(2,128)}, u32[]{:S(2)}) copy-start(f32[1,32,2,256]{3,2,1,0:T(2,128)} %param.16) | copy-start | bytes 196612
